TPU v7x, 32 devices: a whole 2x2x4 slice. The times are simulated.
32 devices in a mesh: inst: 4 (over y, x), head: 8 (over z, core).
Axes of the slice: x: 2, y: 2, z: 4, core: 2. Of those that a mesh axis runs over, the one named last changes fastest.
Arguments:
- old_keys: bfloat16 [512, 16, 64, 128], P('inst', 'head'), may hold values from -6 to 6
- old_values: bfloat16 [512, 16, 64, 128], P('inst', 'head'), may hold values from -6 to 6
- old_block: int32 [512], P('inst'), may hold values from -1 to 127, as said below
- new_slot: int32 [128], replicated, may hold values from 0 to 127, as said below
- lengths: int32 [64], replicated, may hold values from 1 to 8192, as said below
- queries: bfloat16 [64, 16, 8192], P(None, None, 'head'), may hold values from -240 to 240
- draft_keys: bfloat16 [64, 16, 1024], P('inst'), may hold values from -6 to 6
- draft_values: bfloat16 [64, 16, 1024], P('inst'), may hold values from -6 to 6
Outputs:
- moved_keys: bfloat16 [128, 16, 64, 128], P('inst', 'head')
- moved_values: bfloat16 [128, 16, 64, 128], P('inst', 'head')
- attended: bfloat16 [64, 16, 8192], P(None, None, 'head')
Inputs may be any that keep to these rules, and one draw needn't show every extreme that they name: ceil(lengths / 128) summed over the requests is exactly 128; the longest request has exactly 8192 tokens. `old_block`: every block 0 to 127 stands in exactly one old slot; the blocks fill all slots of 1 instances and all other slots hold -1. A permutation; block g goes to instance new_slot[g] // 32. At most 32 blocks go from one old instance to one new one, and in every draw some new instance receives all its 32 blocks from a single old instance.
All inputs are finite; a program needn't handle non-finite values.
Results may differ from a plain program's by a relative error of at most 0.004.
Values may be sent and summed in bfloat16 or wider, within the bound.
A program may use at most 64 MiB of HBM per device.

v0:
```python
import math

import jax
import jax.numpy as jnp
from jax import lax
from jax.sharding import PartitionSpec as P

GROUP = 8
BLK = 128
DRAFT = 16


masked = -1e30


def partner_2(block, axis, stride):
    count = lax.axis_size(axis)
    route = []
    for low in range(count):
        high = low | 1 << stride
        if high != low and high < count:
            route += [(low, high), (high, low)]
    return lax.ppermute(block, axis, route)


def join_partials(earlier, later):
    raised = jnp.maximum(earlier[0], later[0])
    keep_early = jnp.exp(earlier[0] - raised)
    keep_late = jnp.exp(later[0] - raised)
    totals = earlier[1] * keep_early + later[1] * keep_late
    weighted = earlier[2] * keep_early[..., None] + later[2] * keep_late[..., None]
    return (raised, totals, weighted)


def cache_partial(key_cache, value_cache, block_list, lengths, grouped, head_base):
    slot_count, entries, half_len, head_dim = key_cache.shape
    requests, qcount, _ = grouped.shape
    inv_root = 1.0 / math.sqrt(head_dim)
    counts = (lengths + BLK - 1) // BLK
    starts = jnp.cumsum(counts) - counts
    filled = block_list >= 0
    block_owner_list = (
        jnp.sum((starts[None, :] <= block_list[:, None]).astype(jnp.int32), axis=1) - 1
    )
    block_owner_list = jnp.clip(block_owner_list, 0, requests - 1)
    offset = block_list - starts[block_owner_list]
    halves = (head_base + jnp.arange(entries, dtype=jnp.int32)) % 2
    within = (halves[:, None] * half_len + jnp.arange(half_len, dtype=jnp.int32)[None, :]).reshape(
        entries * half_len
    )
    positions = offset[:, None] * BLK + within[None, :]
    usable = filled[:, None] & (positions < lengths[block_owner_list][:, None])
    stride = math.gcd(slot_count, 64)
    nsteps = slot_count // stride
    token_count = entries * half_len
    key_rows_all = key_cache.reshape(nsteps, stride, token_count, head_dim)
    value_rows_all = value_cache.reshape(nsteps, stride, token_count, head_dim)
    request_ids = jnp.arange(requests, dtype=jnp.int32)

    def advance(state_now, pieces):
        peaks, totals, weighted = state_now
        key_rows, value_rows, rows_owner, rows_filled, rows_usable = pieces
        picked = grouped[rows_owner]
        scores = (
            jnp.einsum("sqd,std->sqt", picked, key_rows, preferred_element_type=jnp.float32)
            * inv_root
        )
        scores = jnp.where(rows_usable[:, None, :], scores, masked)
        belongs = (rows_owner[:, None] == request_ids[None, :]) & rows_filled[:, None]
        slot_peaks = jnp.max(scores, axis=-1)
        block_peak = jnp.max(jnp.where(belongs[:, :, None], slot_peaks[:, None, :], masked), axis=0)
        raised = jnp.maximum(peaks, block_peak)
        weights = jnp.where(
            rows_usable[:, None, :], jnp.exp(scores - raised[rows_owner][:, :, None]), 0.0
        )
        belongs_f = belongs.astype(jnp.float32)
        row_sums = jnp.dot(
            belongs_f.T,
            jnp.sum(weights, axis=-1),
            precision=lax.Precision.HIGHEST,
            preferred_element_type=jnp.float32,
        )
        blended = jnp.einsum(
            "sqt,std->sqd",
            weights.astype(jnp.bfloat16),
            value_rows,
            preferred_element_type=jnp.float32,
        )
        gathered = jnp.einsum("sr,sqd->rqd", belongs_f, blended, precision=lax.Precision.HIGHEST)
        rescale = jnp.exp(peaks - raised)
        return (
            (raised, totals * rescale + row_sums, weighted * rescale[..., None] + gathered),
            None,
        )

    start_state = (
        jnp.full((requests, qcount), masked, jnp.float32),
        jnp.zeros((requests, qcount), jnp.float32),
        jnp.zeros((requests, qcount, head_dim), jnp.float32),
    )
    pieces = (
        key_rows_all,
        value_rows_all,
        block_owner_list.reshape(nsteps, stride),
        filled.reshape(nsteps, stride),
        usable.reshape(nsteps, stride, token_count),
    )
    return lax.scan(advance, start_state, pieces)[0]


def draft_partial(grouped, draft_keys, draft_values, current_replica, head_base):
    requests, qcount, head_dim = grouped.shape
    per_token = qcount // DRAFT
    rows_loc = draft_keys.shape[0]
    kv_head = head_base // 2
    own_keys = lax.dynamic_slice_in_dim(draft_keys, kv_head * head_dim, head_dim, 2)
    own_vals = lax.dynamic_slice_in_dim(draft_values, kv_head * head_dim, head_dim, 2)
    own_q = lax.dynamic_slice_in_dim(grouped, current_replica * rows_loc, rows_loc, 0).reshape(
        rows_loc, DRAFT, per_token, head_dim
    )
    inv_root = 1.0 / math.sqrt(head_dim)
    scores = (
        jnp.einsum("rigd,rjd->rigj", own_q, own_keys, preferred_element_type=jnp.float32) * inv_root
    )
    causal = jnp.arange(DRAFT)[None, :] <= jnp.arange(DRAFT)[:, None]
    causal_flat = jnp.broadcast_to(causal[:, None, :], (DRAFT, per_token, DRAFT)).reshape(
        qcount, DRAFT
    )
    scores = jnp.where(causal_flat, scores.reshape(rows_loc, qcount, DRAFT), masked)
    peaks = jnp.max(scores, axis=-1)
    weights = jnp.where(causal_flat, jnp.exp(scores - peaks[..., None]), 0.0)
    totals = jnp.sum(weights, axis=-1)
    weighted = jnp.einsum(
        "rqj,rjd->rqd", weights.astype(jnp.bfloat16), own_vals, preferred_element_type=jnp.float32
    )
    include = head_base % 2 == 0
    peaks = jnp.where(include, peaks, masked)
    totals = jnp.where(include, totals, 0.0)
    weighted = jnp.where(include, weighted, 0.0)
    first_row = current_replica * rows_loc
    full_peaks = lax.dynamic_update_slice_in_dim(
        jnp.full((requests, qcount), masked, jnp.float32), peaks, first_row, 0
    )
    full_totals = lax.dynamic_update_slice_in_dim(
        jnp.zeros((requests, qcount), jnp.float32), totals, first_row, 0
    )
    full_weighted = lax.dynamic_update_slice_in_dim(
        jnp.zeros((requests, qcount, head_dim), jnp.float32), weighted, first_row, 0
    )
    return (full_peaks, full_totals, full_weighted)


def shards(old_keys, old_values, old_block, new_slot, lengths, queries, draft_keys, draft_values):
    replica_count = lax.axis_size("inst")
    current_replica = lax.axis_index("inst")
    me_head = lax.axis_index("head")
    entries = old_keys.shape[1]
    head_dim = old_keys.shape[3]
    head_base = me_head * entries
    block_capacity = new_slot.shape[0]
    slots_per_replica = block_capacity // replica_count
    destination_replica = jnp.where(
        old_block >= 0, new_slot[jnp.clip(old_block, 0, block_capacity - 1)], block_capacity
    )
    trailing_tokens = old_keys.shape[1:]
    outgoing_keys = (
        jnp.zeros((block_capacity,) + trailing_tokens, old_keys.dtype)
        .at[destination_replica]
        .set(old_keys, mode="drop")
    )
    outgoing_values = (
        jnp.zeros((block_capacity,) + trailing_tokens, old_values.dtype)
        .at[destination_replica]
        .set(old_values, mode="drop")
    )
    outgoing_keys = outgoing_keys.reshape((replica_count, slots_per_replica) + trailing_tokens)
    outgoing_values = outgoing_values.reshape((replica_count, slots_per_replica) + trailing_tokens)
    inbox_k, inbox_v = (
        lax.all_to_all(outgoing_keys, "inst", split_axis=0, concat_axis=0, tiled=True),
        lax.all_to_all(outgoing_values, "inst", split_axis=0, concat_axis=0, tiled=True),
    )
    moved_keys = jnp.sum(inbox_k, axis=0)
    moved_values = jnp.sum(inbox_v, axis=0)
    local_heads = queries.shape[2] // head_dim
    requests = queries.shape[0]
    locally_present = (
        jnp.zeros((block_capacity,), jnp.int32)
        .at[new_slot]
        .set(jnp.arange(block_capacity, dtype=jnp.int32))
    )
    block_list = lax.dynamic_slice_in_dim(
        locally_present, current_replica * slots_per_replica, slots_per_replica
    )
    split_tokens = False
    if local_heads < GROUP:
        is_lower = me_head % 2 == 0
        partner = partner_2(queries, "head", 0)
        grouped = jnp.where(
            is_lower,
            jnp.concatenate([queries, partner], axis=2),
            jnp.concatenate([partner, queries], axis=2),
        )
        split_tokens = True
    else:
        grouped = queries
    qcount = grouped.shape[2] // head_dim
    grouped = grouped.reshape(requests, DRAFT * qcount, head_dim)
    cached = cache_partial(moved_keys, moved_values, block_list, lengths, grouped, head_base)
    drafted = draft_partial(grouped, draft_keys, draft_values, current_replica, head_base)
    peaks, totals, weighted = join_partials(cached, drafted)
    if split_tokens:
        peaks = peaks.reshape(requests, DRAFT, 2, local_heads)
        totals = totals.reshape(requests, DRAFT, 2, local_heads)
        weighted = weighted.reshape(requests, DRAFT, 2, local_heads, head_dim)
        is_first = me_head % 2 == 0
        own_peaks = jnp.where(is_first, peaks[:, :, 0], peaks[:, :, 1])
        own_totals = jnp.where(is_first, totals[:, :, 0], totals[:, :, 1])
        own_weighted = jnp.where(is_first, weighted[:, :, 0], weighted[:, :, 1])
        other_peaks = jnp.where(is_first, peaks[:, :, 1], peaks[:, :, 0])
        other_totals = jnp.where(is_first, totals[:, :, 1], totals[:, :, 0])
        other_weighted = jnp.where(is_first, weighted[:, :, 1], weighted[:, :, 0])
        received = partner_2((other_peaks, other_totals, other_weighted), "head", 0)
        peaks, totals, weighted = join_partials((own_peaks, own_totals, own_weighted), received)
    else:
        peaks = peaks.reshape(requests, DRAFT, local_heads)
        totals = totals.reshape(requests, DRAFT, local_heads)
        weighted = weighted.reshape(requests, DRAFT, local_heads, head_dim)
    top_score = lax.pmax(peaks, "inst")
    factor = jnp.exp(peaks - top_score)
    totals, weighted = lax.psum((totals * factor, weighted * factor[..., None]), "inst")
    attended = (
        (weighted / totals[..., None])
        .astype(jnp.bfloat16)
        .reshape(requests, DRAFT, local_heads * head_dim)
    )
    return (moved_keys, moved_values, attended)


def solution(mesh):
    placed = (
        P("inst", "head", None, None),
        P("inst", "head", None, None),
        P("inst"),
        P(),
        P(),
        P(None, None, "head"),
        P("inst", None, None),
        P("inst", None, None),
    )
    return jax.shard_map(
        shards,
        mesh=mesh,
        in_specs=placed,
        out_specs=(
            P("inst", "head", None, None),
            P("inst", "head", None, None),
            P(None, None, "head"),
        ),
        check_vma=False,
    )
```

profile of v0, /device:TPU:0, one launch (start us, length us, event | category | flops | bytes accessed | tf_op | source)
XLA Modules:
  0.0 284.8 jit_solution(17982491135180014713)
XLA Ops:
  7.2 0.0 copy-start
  7.2 0.7 compare_select_fusion.3
  7.9 1.6 gather_fusion
  9.5 0.7 compare_select_fusion.1
  10.2 3.0 %broadcast.212.clone = bf16[128,2,64,128]{3,2,1,0:T(8,128)(2,1)} broadcast(bf16[]{:T(256)} %constant.70.clone.1), dimensions={} | broadcast | bytes 4194306 | tf_op jit(solution)/shard_map/broadcast.23
  13.2 19.4 %scatter_fusion = bf16[128,2,64,128]{3,2,1,0:T(8,128)(2,1)} fusion(bf16[128,2,64,128]{3,2,1,0:T(8,128)(2,1)} %broadcast.212.clone, s32[128]{0:T(128)S(1)} %get-tuple-element.50, bf16[128,2,64,128]{3,2,1,0:T(8,128)(2,1)} %param.8), kind=kCustom, calls=%fused_computation.5 | custom fusion | bytes 12583424 | tf_op jit(solution)/shard_map/scatter | solution.py:169
  32.6 5.0 %all-to-all-start = ((bf16[4,32,2,64,128]{4,3,2,1,0:T(8,128)(2,1)}), bf16[4,32,2,64,128]{4,3,2,1,0:T(8,128)(2,1)}, u32[]{:S(2)}, u32[]{:S(2)}) async-start(bf16[4,32,2,64,128]{4,3,2,1,0:T(8,128)(2,1)} %bitcast.46), calls=%async_computation | async-start | bytes 8388608 | tf_op jit(solution)/shard_map/all_to_all | solution.py:179
  37.6 0.0 copy-done.1
  37.6 0.1 copy.52
  37.7 0.1 reduce-window.9
  37.8 0.1 reduce.4
  38.0 1.0 scatter_custom_fusion.2
  38.9 0.1 broadcast_compare_fusion
  39.0 0.2 convert_reduce_fusion
  39.2 0.7 gather_fusion.1
  39.9 0.7 gather_fusion.2
  40.7 0.1 iota_add_fusion
  40.8 0.1 add.147
  40.9 0.1 copy.59
  40.9 2.8 reshape.222
  43.8 0.0 copy-start.2
  43.8 1.7 gather_fusion.3
  45.5 0.0 copy-done.2
  45.5 1.5 select_reduce_fusion.2
  47.0 0.1 copy.56
  47.1 3.0 %broadcast.212.clone.1 = bf16[128,2,64,128]{3,2,1,0:T(8,128)(2,1)} broadcast(bf16[]{:T(256)} %constant.70.clone.1), dimensions={} | broadcast | bytes 4194306 | tf_op jit(solution)/shard_map/broadcast.23
  50.2 19.4 %scatter_fusion.1 = bf16[128,2,64,128]{3,2,1,0:T(8,128)(2,1)} fusion(bf16[128,2,64,128]{3,2,1,0:T(8,128)(2,1)} %broadcast.212.clone.1, s32[128]{0:T(128)S(1)} %get-tuple-element.50, bf16[128,2,64,128]{3,2,1,0:T(8,128)(2,1)} %param.9), kind=kCustom, calls=%fused_computation.6 | custom fusion | bytes 12583424 | tf_op jit(solution)/shard_map/scatter | solution.py:174
  69.5 0.7 select_reduce_fusion
  70.2 15.8 %all-to-all-done = bf16[4,32,2,64,128]{4,3,2,1,0:T(8,128)(2,1)} async-done(((bf16[4,32,2,64,128]{4,3,2,1,0:T(8,128)(2,1)}), bf16[4,32,2,64,128]{4,3,2,1,0:T(8,128)(2,1)}, u32[]{:S(2)}, u32[]{:S(2)}) %all-to-all-start) | async-done | bytes 4194336 | tf_op jit(solution)/shard_map/all_to_all | solution.py:179
  85.9 4.8 %all-to-all-start.1 = ((bf16[4,32,2,64,128]{4,3,2,1,0:T(8,128)(2,1)}), bf16[4,32,2,64,128]{4,3,2,1,0:T(8,128)(2,1)}, u32[]{:S(2)}, u32[]{:S(2)}) async-start(bf16[4,32,2,64,128]{4,3,2,1,0:T(8,128)(2,1)} %bitcast.45), calls=%async_computation.1 | async-start | bytes 8388608 | tf_op jit(solution)/shard_map/all_to_all | solution.py:180
  90.8 0.0 all-reduce.2.cloned.1.call-start
  90.9 0.1 copy.65
  91.0 0.1 copy.66
  91.0 0.1 copy.57
  91.1 0.3 copy.60
  91.5 0.1 fusion.24
  91.5 0.1 fusion.25
  91.6 0.0 copy-done
  91.7 0.4 fusion.16
  92.0 2.5 broadcast.224
  94.5 1.7 fusion.8
  96.2 4.4 %reduce_sum.52 = bf16[32,2,64,128]{3,2,1,0:T(8,128)(2,1)} reduce(bf16[4,32,2,64,128]{4,3,2,1,0:T(8,128)(2,1)} %all-to-all-done, bf16[]{:T(256)} %constant.70.clone.1), dimensions={0}, to_apply=%region_1.2 | reduce | flops 1572864 | bytes 5242882 | tf_op jit(solution)/shard_map/reduce_sum | solution.py:182
  100.6 3.1 %fusion.1 = (f32[32,128]{1,0:T(8,128)S(1)}, f32[32,128,128]{1,2,0:T(8,128)S(1)}) fusion(pred[32,128]{1,0:T(8,128)(4,1)S(1)} %fusion.25, bf16[32,128,128]{2,1,0:T(8,128)(2,1)} %gather_fusion.3, bf16[32,128,128]{2,1,0:T(8,128)(2,1)} %bitcast.49), kind=kOutput, calls=%fused_computation.14 | convolution fusion | flops 135786496 | bytes 4214784 | tf_op jit(solution)/shard_map/while/body/eval_jaxpr/sqd,std->sqt/dot_general | solution.py:65
  103.7 0.3 select_reduce_fusion.1
  104.1 0.6 gather_fusion.4
  104.7 0.1 copy.64
  104.8 0.1 copy.63
  104.9 0.1 copy.58
  105.0 0.9 fusion.2
  105.9 0.3 fusion.5
  106.2 0.1 copy.67
  106.3 0.1 copy.53
  106.4 42.4 %pmax.7 = f32[64,16,8]{0,2,1:T(8,128)S(1)} all-reduce(f32[64,16,8]{0,2,1:T(8,128)S(1)} %bitcast.51), channel_id=1, replica_groups=mesh['inst'=4,'head'=8] {'inst'}, use_global_device_ids=true, to_apply=%region_10.11 | all-reduce | flops 8192 | bytes 65536 | tf_op jit(solution)/shard_map/pmax | solution.py:228
  148.8 0.0 all-to-all-done.1
  148.8 4.4 %reduce_sum.53 = bf16[32,2,64,128]{3,2,1,0:T(8,128)(2,1)} reduce(bf16[4,32,2,64,128]{4,3,2,1,0:T(8,128)(2,1)} %all-to-all-done.1, bf16[]{:T(256)} %constant.70.clone.1), dimensions={0}, to_apply=%region_3.4 | reduce | flops 1572864 | bytes 5242882 | tf_op jit(solution)/shard_map/reduce_sum | solution.py:183
  153.2 3.3 %fusion.6 = f32[32,128,128]{2,1,0:T(8,128)S(1)} fusion(bf16[32,128,128]{2,1,0:T(8,128)(2,1)} %bitcast.50, f32[32,128,128]{1,2,0:T(8,128)S(1)} %get-tuple-element.48, f32[32,128]{1,0:T(8,128)S(1)} %gather_fusion.4, pred[32,128]{1,0:T(8,128)(4,1)S(1)} %fusion.25), kind=kOutput, calls=%fused_computation.21 | convolution fusion | flops 136839168 | bytes 5263360 | tf_op jit(solution)/shard_map/while/body/eval_jaxpr/sqt,std->sqd/dot_general | solution.py:83
  156.5 7.3 %multiply_add_fusion = f32[64,128,128]{2,0,1:T(8,128)S(1)} fusion(f32[64,128,128]{2,0,1:T(8,128)} %fusion.8, f32[32,128,128]{2,1,0:T(8,128)S(1)} %fusion.6, f32[64,128]{0,1:T(8,128)S(1)} %copy.63, f32[64,128]{0,1:T(8,128)S(1)} %copy.58, f32[64,128]{0,1:T(8,128)S(1)} %copy.53, s32[32]{0:T(128)S(1)} %add_clamp_fusion, pred[32]{0:T(512)(128)(4,1)S(1)} %get-tuple-element.27), kind=kOutput, calls=%fused_computation.9 | convolution fusion | flops 406851584 | bytes 10584224 | tf_op jit(solution)/shard_map/while/body/eval_jaxpr/sr,sqd->rqd/dot_general | solution.py:89
  163.9 2.6 broadcast_multiply_fusion
  166.5 0.0 all-reduce.2.cloned.1.call-update
  166.5 17.4 %psum.15 = f32[64,16,8]{0,2,1:T(8,128)S(1)} all-reduce(f32[64,16,8]{0,2,1:T(8,128)S(1)} %get-tuple-element.25), channel_id=1, replica_groups=mesh['inst'=4,'head'=8] {'inst'}, use_global_device_ids=true, to_apply=%region_14.15 | all-reduce | flops 8192 | bytes 65536 | tf_op jit(solution)/shard_map/psum | solution.py:230
  183.9 87.6 %all-reduce.2.cloned.1.call-done = f32[64,16,8,128]{3,0,2,1:T(8,128)} async-done(((f32[64,16,8,128]{3,0,2,1:T(8,128)}), f32[64,16,8,128]{3,0,2,1:T(8,128)}) %all-reduce.2.cloned.1.call-update) | async-done | bytes 4194320 | tf_op jit(solution)/shard_map/psum | solution.py:230
  271.4 2.9 %divide_convert_fusion = bf16[64,16,8,128]{3,0,2,1:T(8,128)(2,1)S(1)} fusion(f32[64,16,8,128]{3,0,2,1:T(8,128)} %all-reduce.2.cloned.1.call-done, f32[64,16,8]{0,2,1:T(8,128)S(1)} %psum.15), kind=kLoop, calls=%fused_computation.8 | loop fusion | flops 2097152 | bytes 6324224 | tf_op jit(solution)/shard_map/convert_element_type | solution.py:233
  274.3 1.4 copy.68
  275.6 2.3 reshape.229
  (19 shorter events, 0.2 us)
Async XLA Ops:
  7.2 84.5 %copy-start = (bf16[16,16,1024]{2,1,0:T(8,128)(2,1)S(1)}, bf16[16,16,1024]{2,1,0:T(8,128)(2,1)}, u32[]{:S(2)}) copy-start(bf16[16,16,1024]{2,1,0:T(8,128)(2,1)} %param.15) | copy-start | bytes 1572868
  32.6 5.0 %copy-start.1 = (s32[64]{0:T(128)S(1)}, s32[64]{0:T(128)}, u32[]{:S(2)}) copy-start(s32[64]{0:T(128)} %param.12) | copy-start | bytes 772
  32.6 53.3 %all-to-all-start = ((bf16[4,32,2,64,128]{4,3,2,1,0:T(8,128)(2,1)}), bf16[4,32,2,64,128]{4,3,2,1,0:T(8,128)(2,1)}, u32[]{:S(2)}, u32[]{:S(2)}) async-start(bf16[4,32,2,64,128]{4,3,2,1,0:T(8,128)(2,1)} %bitcast.46), calls=%async_computation | async-start | bytes 8388608 | tf_op jit(solution)/shard_map/all_to_all | solution.py:179
  43.8 1.7 copy-start.2
  85.9 62.8 %all-to-all-start.1 = ((bf16[4,32,2,64,128]{4,3,2,1,0:T(8,128)(2,1)}), bf16[4,32,2,64,128]{4,3,2,1,0:T(8,128)(2,1)}, u32[]{:S(2)}, u32[]{:S(2)}) async-start(bf16[4,32,2,64,128]{4,3,2,1,0:T(8,128)(2,1)} %bitcast.45), calls=%async_computation.1 | async-start | bytes 8388608 | tf_op jit(solution)/shard_map/all_to_all | solution.py:180
  90.8 180.6 %all-reduce.2.cloned.1.call-start = ((), (), s32[]{:S(2)}) async-start(), calls=%async_computation.2 | async-start | bytes 8388608 | tf_op jit(solution)/shard_map/psum | solution.py:230
Sparse Core Ops, SparseCore 0:
  166.6 104.7 all-reduce.1
where the time goes:
time: 286 us; the launch traced here: 285 us
  waiting for transfers between devices  103 us (36%)
  local copies, waits for them, and re-layouts  61.4 us (21%)
  blocking collectives  59.8 us (21%)
  other arithmetic  20.1 us (7%)
  matrix products  15.9 us (6%)
  between operations  14.4 us (5%)
  starting transfers between devices  9.87 us (3%)
    psum x1, waiting for transfers between devices, shards(): lax.psum((totals * factor, weighted * factor[..., None]), 'inst')  87.6 us
    pmax x1, blocking collectives, shards(): top_score = lax.pmax(peaks, 'inst')  42.4 us
    scatter x1, local copies, waits for them, and re-layouts, shards(): outgoing_keys = jnp.zeros((block_capacity,) + trailing_tokens, old_keys.d...  19.4 us
    scatter x1, local copies, waits for them, and re-layouts, shards(): outgoing_values = jnp.zeros((block_capacity,) + trailing_tokens, old_valu...  19.4 us
    psum x1, blocking collectives, shards(): lax.psum((totals * factor, weighted * factor[..., None]), 'inst')  17.4 us
    all_to_all x1, waiting for transfers between devices, shards(): lax.all_to_all(outgoing_keys, 'inst', split_axis=0, concat_axis=0, tiled=...  15.8 us
    another operation x6, local copies, waits for them, and re-layouts  8.66 us
    dot_general x1, matrix products, advance(): jnp.einsum('sr,sqd->rqd', belongs_f, blended, precision=lax.Precision.HIG...  7.31 us
  transfers between devices with their start and end apart: 3, of which 2 were waited for; matrix products, arithmetic and copies ran while one was open for 17% of the time, Pallas kernels for 0%

commit v1 on v0

--- a/solution.py
+++ b/solution.py
@@ -1,8 +1,11 @@
+import functools
 import math
 
 import jax
 import jax.numpy as jnp
 from jax import lax
+from jax.experimental import pallas as pl
+from jax.experimental.pallas import tpu as pltpu
 from jax.sharding import PartitionSpec as P
 
 GROUP = 8
@@ -150,7 +153,7 @@
     return (full_peaks, full_totals, full_weighted)
 
 
-def shards(old_keys, old_values, old_block, new_slot, lengths, queries, draft_keys, draft_values):
+def general_shards(old_keys, old_values, old_block, new_slot, lengths, queries, draft_keys, draft_values):
     replica_count = lax.axis_size("inst")
     current_replica = lax.axis_index("inst")
     me_head = lax.axis_index("head")
@@ -236,6 +239,462 @@
     return (moved_keys, moved_values, attended)
 
 
+UNROLL = 4
+SEND_SPLIT = 2
+
+
+def flag_kernel(n, flag_ref, out_ref, send_sem, recv_sem):
+    me = lax.axis_index("inst")
+    barrier = pltpu.get_barrier_semaphore()
+    for step in range(1, n):
+        pl.semaphore_signal(
+            barrier,
+            inc=1,
+            device_id={"inst": lax.rem(me + step, n)},
+            device_id_type=pl.DeviceIdType.MESH,
+        )
+    pl.semaphore_wait(barrier, n - 1)
+    copies = []
+    for step in range(1, n):
+        copy = pltpu.make_async_remote_copy(
+            src_ref=flag_ref,
+            dst_ref=out_ref.at[step],
+            send_sem=send_sem.at[step],
+            recv_sem=recv_sem.at[step],
+            device_id={"inst": lax.rem(me + step, n)},
+            device_id_type=pl.DeviceIdType.MESH,
+        )
+        copy.start()
+        copies.append(copy)
+    out_ref[0] = flag_ref[...]
+    for copy in copies:
+        copy.wait()
+
+
+def find_holder(old_block, n):
+    me = lax.axis_index("inst")
+    mine = jnp.broadcast_to((jnp.max(old_block) >= 0).astype(jnp.int32), (8, 128))
+    flags = pl.pallas_call(
+        functools.partial(flag_kernel, n),
+        out_shape=jax.ShapeDtypeStruct((n, 8, 128), jnp.int32),
+        in_specs=[pl.BlockSpec(memory_space=pltpu.VMEM)],
+        out_specs=pl.BlockSpec(memory_space=pltpu.VMEM),
+        scratch_shapes=[pltpu.SemaphoreType.DMA((n,)), pltpu.SemaphoreType.DMA((n,))],
+        compiler_params=pltpu.CompilerParams(collective_id=0, has_side_effects=True),
+    )(mine)
+    origin = (me - jnp.arange(n, dtype=jnp.int32) + n) % n
+    return jnp.sum(origin * flags[:, 0, 0])
+
+
+def tables(old_block, new_slot, lengths):
+    blocks = new_slot.shape[0]
+    requests = lengths.shape[0]
+    ids = jnp.arange(blocks, dtype=jnp.int32)
+    spots = jnp.arange(old_block.shape[0], dtype=jnp.int32)
+    source = jnp.sum(jnp.where(old_block[None, :] == ids[:, None], spots[None, :], 0), axis=1)
+    placed = jnp.sum(jnp.where(old_block[:, None] == ids[None, :], new_slot[None, :] + 1, 0), axis=1) - 1
+    by_slot = jnp.sum(jnp.where(placed[None, :] == ids[:, None], spots[None, :], 0), axis=1)
+    counts = (lengths + BLK - 1) // BLK
+    reqs = jnp.arange(requests, dtype=jnp.int32)
+    ends = jnp.sum(jnp.where(reqs[None, :] <= reqs[:, None], counts[None, :], 0), axis=1)
+    starts = ends - counts
+    inside = (starts[None, :] <= ids[:, None]) & (ids[:, None] < ends[None, :])
+    owner = jnp.sum(jnp.where(inside, reqs[None, :], 0), axis=1)
+    left = lengths[None, :] - (ids[:, None] - starts[None, :]) * BLK
+    live = jnp.minimum(jnp.sum(jnp.where(inside, left, 0), axis=1), BLK)
+    first = jnp.sum(jnp.where(inside & (starts[None, :] == ids[:, None]), 1, 0), axis=1)
+    last = jnp.pad(ends - 1, (0, blocks - requests))
+    return jnp.stack([source, by_slot, owner, live, first, last])
+
+
+def fused_kernel(
+    holder,
+    tab,
+    keys_hbm,
+    values_hbm,
+    queries_hbm,
+    dkeys_hbm,
+    dvals_hbm,
+    mk_out,
+    mv_out,
+    att_out,
+    kbuf,
+    vbuf,
+    qbuf,
+    dk,
+    dv,
+    send_k,
+    send_v,
+    relay,
+    per_block,
+    att,
+    m_ref,
+    l_ref,
+    acc_ref,
+    load_sem,
+    keep_sem,
+    draft_send,
+    draft_recv,
+    blk_send,
+    blk_recv,
+    fwd_send,
+    fwd_recv,
+    att_send,
+    att_recv,
+    pass_send,
+    pass_recv,
+):
+    me = lax.axis_index("inst")
+    head = lax.axis_index("head")
+    mesh_id = pl.DeviceIdType.MESH
+    cross_x, cross_y, far = holder ^ 1, holder ^ 2, holder ^ 3
+    insts = 4
+    blocks = kbuf.shape[0]
+    per_inst = blocks // insts
+    head_dim = kbuf.shape[3]
+    requests = qbuf.shape[0]
+    rows_loc = requests // insts
+    local_heads = qbuf.shape[2] // head_dim
+    units = 4
+    unit = per_inst // units
+    nchunk = 8
+    chunk = requests // nchunk
+    half_chunks = nchunk // 2
+
+    barrier = pltpu.get_barrier_semaphore()
+    for step in range(1, insts):
+        pl.semaphore_signal(
+            barrier, inc=1, device_id={"inst": lax.rem(me + step, insts)}, device_id_type=mesh_id
+        )
+    pl.semaphore_wait(barrier, insts - 1)
+
+    lanes = pl.ds(pl.multiple_of(head * head_dim, head_dim), head_dim)
+
+    def draft_copies(origin):
+        rows = pl.ds(origin * rows_loc, rows_loc)
+        return [
+            pltpu.make_async_remote_copy(
+                src_ref=src.at[:, :, lanes],
+                dst_ref=dst.at[rows],
+                send_sem=draft_send.at[n],
+                recv_sem=draft_recv.at[origin, n],
+                device_id={"inst": holder},
+                device_id_type=mesh_id,
+            )
+            for n, (src, dst) in enumerate(((dkeys_hbm, dk), (dvals_hbm, dv)))
+        ]
+
+    def out_of(n):
+        return (mk_out, mv_out)[n // units].at[pl.ds((n % units) * unit, unit)]
+
+    def staged(inst, n):
+        return (send_k, send_v)[n // units].at[pl.ds(inst * per_inst + (n % units) * unit, unit)]
+
+    def block_copy(inst, n):
+        if inst == far:
+            to = cross_x if n % 2 == 0 else cross_y
+            dst = relay.at[n // 2]
+        else:
+            to = inst
+            dst = out_of(n)
+        return pltpu.make_async_remote_copy(
+            src_ref=staged(inst, n),
+            dst_ref=dst,
+            send_sem=blk_send.at[inst, n],
+            recv_sem=blk_recv.at[inst, n],
+            device_id={"inst": to},
+            device_id_type=mesh_id,
+        )
+
+    def relay_copy(n):
+        return pltpu.make_async_remote_copy(
+            src_ref=relay.at[n // 2],
+            dst_ref=out_of(n),
+            send_sem=fwd_send.at[n],
+            recv_sem=fwd_recv.at[n],
+            device_id={"inst": far},
+            device_id_type=mesh_id,
+        )
+
+    def att_copy(src, c, to, send, recv):
+        rows = pl.ds(c * chunk, chunk)
+        return pltpu.make_async_remote_copy(
+            src_ref=src.at[rows],
+            dst_ref=att_out.at[rows],
+            send_sem=send.at[c],
+            recv_sem=recv.at[c],
+            device_id={"inst": to},
+            device_id_type=mesh_id,
+        )
+
+    def first_hop(c):
+        return att_copy(att, c, cross_x if c < half_chunks else cross_y, att_send, att_recv)
+
+    def second_hop(c):
+        return att_copy(att_out, c, far, pass_send, pass_recv)
+
+    def third_hop(c):
+        return att_copy(
+            att_out, c, cross_y if c < half_chunks else cross_x, att_send, att_recv
+        )
+
+    @pl.when(me == holder)
+    def _():
+        loads = [
+            pltpu.make_async_copy(src, dst, load_sem.at[n])
+            for n, (src, dst) in enumerate(
+                (
+                    (keys_hbm, kbuf),
+                    (values_hbm, vbuf),
+                    (queries_hbm, qbuf),
+                    (dkeys_hbm.at[:, :, lanes], dk.at[pl.ds(holder * rows_loc, rows_loc)]),
+                    (dvals_hbm.at[:, :, lanes], dv.at[pl.ds(holder * rows_loc, rows_loc)]),
+                )
+            )
+        ]
+        for load in loads:
+            load.start()
+
+        def fill(src, dst, inst):
+            def one(i, _):
+                slot = inst * per_inst + i
+                dst[slot] = src[tab[1, slot]]
+                return 0
+
+            lax.fori_loop(0, per_inst, one, 0)
+
+        loads[0].wait()
+        fill(kbuf, send_k, far)
+        fill(kbuf, send_k, cross_x)
+        for n in range(units):
+            block_copy(far, n).start()
+        loads[1].wait()
+        fill(vbuf, send_v, far)
+        fill(kbuf, send_k, cross_y)
+        for n in range(units, 2 * units):
+            block_copy(far, n).start()
+        fill(vbuf, send_v, cross_x)
+        fill(vbuf, send_v, cross_y)
+        for n in range(SEND_SPLIT):
+            block_copy(cross_x, n).start()
+            block_copy(cross_y, n).start()
+        fill(kbuf, send_k, holder)
+        fill(vbuf, send_v, holder)
+
+        for load in loads[2:]:
+            load.wait()
+        for origin in (cross_x, cross_y, far):
+            for copy in draft_copies(origin):
+                copy.wait_recv()
+
+        inv_root = 1.0 / math.sqrt(head_dim)
+        rows = DRAFT * local_heads
+        cols = BLK + DRAFT
+        col = lax.broadcasted_iota(jnp.int32, (rows, cols), 1)
+        row = lax.broadcasted_iota(jnp.int32, (rows, cols), 0)
+        causal = (col >= BLK) & (col - BLK <= row % DRAFT)
+        causal_i = causal.astype(jnp.int32)
+        m_ref[...] = jnp.full(m_ref.shape, masked, jnp.float32)
+        l_ref[...] = jnp.zeros(l_ref.shape, jnp.float32)
+        acc_ref[...] = jnp.zeros(acc_ref.shape, jnp.float32)
+
+        def attend(step, _):
+            parts = []
+            for u in range(UNROLL):
+                g = step * UNROLL + u
+                spot, owner, live, first = tab[0, g], tab[2, g], tab[3, g], tab[4, g]
+                q = qbuf[owner]
+                q = jnp.concatenate(
+                    [q[:, j * head_dim : (j + 1) * head_dim] for j in range(local_heads)], axis=0
+                )
+                k = jnp.concatenate([kbuf[spot].reshape(BLK, head_dim), dk[owner]], axis=0)
+                v = jnp.concatenate([vbuf[spot].reshape(BLK, head_dim), dv[owner]], axis=0)
+                s = (
+                    lax.dot_general(
+                        q, k, (((1,), (1,)), ((), ())), preferred_element_type=jnp.float32
+                    )
+                    * inv_root
+                )
+                usable = (col < live) | (causal_i * first > 0)
+                s = jnp.where(usable, s, masked)
+                m = jnp.max(s, axis=1, keepdims=True)
+                p = jnp.exp(s - m)
+                l = jnp.sum(p, axis=1, keepdims=True)
+                acc = jnp.dot(p.astype(jnp.bfloat16), v, preferred_element_type=jnp.float32)
+                parts.append((g, first, m, l, acc))
+            m_run, l_run, acc_run = m_ref[...], l_ref[...], acc_ref[...]
+            for g, first, m, l, acc in parts:
+                m_run = jnp.where(first > 0, masked, m_run)
+                raised = jnp.maximum(m_run, m)
+                old = jnp.exp(m_run - raised)
+                new = jnp.exp(m - raised)
+                m_run = raised
+                l_run = l_run * old + l * new
+                acc_run = acc_run * old + acc * new
+                out = (acc_run / l_run).astype(jnp.bfloat16)
+                for j in range(local_heads):
+                    per_block[g, :, j * head_dim : (j + 1) * head_dim] = out[
+                        j * DRAFT : (j + 1) * DRAFT
+                    ]
+            m_ref[...], l_ref[...], acc_ref[...] = m_run, l_run, acc_run
+            return 0
+
+        lax.fori_loop(0, blocks // UNROLL, attend, 0)
+
+        def pick(r, _):
+            att[r] = per_block[tab[5, r]]
+            return 0
+
+        lax.fori_loop(0, requests, pick, 0)
+        keeps = [
+            pltpu.make_async_copy(staged(holder, n), out_of(n), keep_sem.at[n])
+            for n in range(2 * units)
+        ]
+        for keep in keeps:
+            keep.start()
+        for c in range(half_chunks):
+            first_hop(c).start()
+            first_hop(c + half_chunks).start()
+        for n in range(SEND_SPLIT, 2 * units):
+            block_copy(cross_x, n).start()
+            block_copy(cross_y, n).start()
+        own = pltpu.make_async_copy(att, att_out, load_sem.at[5])
+        own.start()
+        for keep in keeps:
+            keep.wait()
+        own.wait()
+        for n in range(2 * units):
+            for inst in (far, cross_x, cross_y):
+                block_copy(inst, n).wait_send()
+        for c in range(nchunk):
+            first_hop(c).wait_send()
+
+    @pl.when(me != holder)
+    def _():
+        for copy in draft_copies(me):
+            copy.start()
+
+    for side, relayed, mine, theirs in (
+        (cross_x, range(0, 2 * units, 2), range(half_chunks), range(half_chunks, nchunk)),
+        (cross_y, range(1, 2 * units, 2), range(half_chunks, nchunk), range(half_chunks)),
+    ):
+
+        @pl.when(me == side)
+        def _(side=side, relayed=relayed, mine=mine, theirs=theirs):
+            for n in relayed:
+                block_copy(far, n).wait_recv()
+                relay_copy(n).start()
+            for c in mine:
+                first_hop(c).wait_recv()
+                second_hop(c).start()
+            for n in range(2 * units):
+                block_copy(side, n).wait_recv()
+            for c in theirs:
+                third_hop(c).wait_recv()
+            for n in relayed:
+                relay_copy(n).wait_send()
+            for c in mine:
+                second_hop(c).wait_send()
+
+    @pl.when(me == far)
+    def _():
+        for n in range(2 * units):
+            relay_copy(n).wait_recv()
+        for c in range(half_chunks):
+            for half in (c, c + half_chunks):
+                second_hop(half).wait_recv()
+                third_hop(half).start()
+        for c in range(nchunk):
+            third_hop(c).wait_send()
+
+    @pl.when(me != holder)
+    def _():
+        for copy in draft_copies(me):
+            copy.wait_send()
+
+
+def fused(holder, tab, old_keys, old_values, queries, draft_keys, draft_values):
+    blocks = old_keys.shape[0]
+    per_inst = blocks // 4
+    requests, draft, width = queries.shape
+    head_dim = old_keys.shape[3]
+    rows = draft * (width // head_dim)
+    block = old_keys.shape[1:]
+    units = 4
+    dma = pltpu.SemaphoreType.DMA
+    any_space = pl.BlockSpec(memory_space=pl.ANY)
+    bf = jnp.bfloat16
+    return pl.pallas_call(
+        functools.partial(fused_kernel, holder),
+        out_shape=(
+            jax.ShapeDtypeStruct((per_inst,) + block, bf),
+            jax.ShapeDtypeStruct((per_inst,) + block, bf),
+            jax.ShapeDtypeStruct(queries.shape, bf),
+        ),
+        in_specs=[pl.BlockSpec(memory_space=pltpu.SMEM)] + [any_space] * 5,
+        out_specs=(any_space,) * 3,
+        scratch_shapes=[
+            pltpu.VMEM((blocks,) + block, bf),
+            pltpu.VMEM((blocks,) + block, bf),
+            pltpu.VMEM(queries.shape, bf),
+            pltpu.VMEM((requests, draft, head_dim), bf),
+            pltpu.VMEM((requests, draft, head_dim), bf),
+            pltpu.VMEM((blocks,) + block, bf),
+            pltpu.VMEM((blocks,) + block, bf),
+            pltpu.VMEM((units, per_inst // units) + block, bf),
+            pltpu.VMEM((blocks, draft, width), bf),
+            pltpu.VMEM(queries.shape, bf),
+            pltpu.VMEM((rows, head_dim), jnp.float32),
+            pltpu.VMEM((rows, head_dim), jnp.float32),
+            pltpu.VMEM((rows, head_dim), jnp.float32),
+            dma((6,)),
+            dma((2 * units,)),
+            dma((2,)),
+            dma((4, 2)),
+            dma((4, 2 * units)),
+            dma((4, 2 * units)),
+            dma((2 * units,)),
+            dma((2 * units,)),
+            dma((8,)),
+            dma((8,)),
+            dma((8,)),
+            dma((8,)),
+        ],
+        compiler_params=pltpu.CompilerParams(
+            collective_id=1 + holder, has_side_effects=True, vmem_limit_bytes=60 * 1024 * 1024
+        ),
+    )(tab, old_keys, old_values, queries, draft_keys, draft_values)
+
+
+def shards(old_keys, old_values, old_block, new_slot, lengths, queries, draft_keys, draft_values):
+    insts = lax.axis_size("inst")
+    plain = (
+        insts == 4
+        and old_block.shape[0] == new_slot.shape[0]
+        and old_keys.shape[1] * old_keys.shape[2] == BLK
+        and queries.shape[2] // old_keys.shape[3] == GROUP
+        and lengths.shape[0] % 8 == 0
+        and new_slot.shape[0] % 16 == 0
+        and lengths.shape[0] <= new_slot.shape[0]
+    )
+    if not plain:
+        return general_shards(
+            old_keys, old_values, old_block, new_slot, lengths, queries, draft_keys, draft_values
+        )
+    holder = find_holder(old_block, insts)
+    tab = tables(old_block, new_slot, lengths)
+    return lax.switch(
+        holder,
+        [functools.partial(fused, h) for h in range(insts)],
+        tab,
+        old_keys,
+        old_values,
+        queries,
+        draft_keys,
+        draft_values,
+    )
+
+
 def solution(mesh):
     placed = (
         P("inst", "head", None, None),

time: 286 us -> 117 us (0.41)
  Pallas kernels: 0 us -> 103 us
  waiting for transfers between devices: 103 us -> 0 us
  blocking collectives: 59.8 us -> 0 us
  local copies, waits for them, and re-layouts: 61.4 us -> 5.38 us
  matrix products: 15.9 us -> 0 us
  other arithmetic: 20.1 us -> 5.84 us
  between operations: 14.4 us -> 1.99 us
  starting transfers between devices: 9.87 us -> 0 us
    pallas_call x0 -> x2, Pallas kernels: none -> 103 us  [the longest x1 95.7 us: fused(): pl.pallas_call(functools.partial(fused_kernel, holder), out_shape=(jax.Sh...]
    psum x1 -> x0, waiting for transfers between devices: 87.6 us -> none  [shards(): lax.psum((totals * factor, weighted * factor[..., None]), 'inst')]
    pmax x1 -> x0, blocking collectives: 42.4 us -> none  [shards(): top_score = lax.pmax(peaks, 'inst')]
    scatter x3 -> x0, local copies, waits for them, and re-layouts: 39.7 us -> none  [the longest x1 19.4 us: shards(): outgoing_keys = jnp.zeros((block_capacity,) + trailing_tokens, old_keys.d...]
    psum x1 -> x0, blocking collectives: 17.4 us -> none  [shards(): lax.psum((totals * factor, weighted * factor[..., None]), 'inst')]
    dot_general x6 -> x0, matrix products: 15.9 us -> none  [the longest x1 7.31 us: advance(): jnp.einsum('sr,sqd->rqd', belongs_f, blended, precision=lax.Precision.HIG...]
    all_to_all x2 -> x0, waiting for transfers between devices: 15.8 us -> none  [the longest x1 15.8 us: shards(): lax.all_to_all(outgoing_keys, 'inst', split_axis=0, concat_axis=0, tiled=...]
    all_to_all x2 -> x0, starting transfers between devices: 9.83 us -> none  [the longest x1 4.99 us: shards(): lax.all_to_all(outgoing_keys, 'inst', split_axis=0, concat_axis=0, tiled=...]
  transfers between devices with their start and end apart: 3 -> 0, of which waited for: 2 -> 0; matrix products, arithmetic and copies ran while one was open for 17% -> 0% of each run, Pallas kernels for 0% -> 0%
where the time goes in v1:
time: 117 us; the launch traced here: 116 us
  Pallas kernels  103 us (88%)
  other arithmetic  5.84 us (5%)
  local copies, waits for them, and re-layouts  5.38 us (5%)
  between operations  1.99 us (2%)
    pallas_call x1, Pallas kernels, fused(): pl.pallas_call(functools.partial(fused_kernel, holder), out_shape=(jax.Sh...  95.7 us
    pallas_call x1, Pallas kernels, find_holder(): pl.pallas_call(functools.partial(flag_kernel, n), out_shape=jax.ShapeDtyp...  7.46 us
    unnamed x5, local copies, waits for them, and re-layouts  3.88 us

profile of v1, /device:TPU:0, one launch (start us, length us, event | category | flops | bytes accessed | tf_op | source)
XLA Modules:
  0.0 116.4 jit_solution(7175936979523320352)
XLA Ops:
  0.6 1.3 %reduce_max.9 = s32[]{:T(128)} reduce(s32[128]{0:T(128)} %param.14, s32[]{:T(128)} %constant.46.clone.1), dimensions={0}, to_apply=%region_0.0 | reduce | flops 127 | bytes 520 | tf_op jit(solution)/shard_map/reduce_max | solution.py:276
  2.6 0.7 broadcast_add_fusion.2
  3.2 0.7 and_select_fusion
  3.9 0.1 select_reduce_fusion.6
  4.0 0.9 select_reduce_fusion.1
  4.9 0.1 select_reduce_fusion
  5.1 0.7 broadcast_add_fusion
  5.7 0.8 select_reduce_fusion.3
  6.5 0.6 broadcast_in_dim.83.flag_ref
  7.1 7.5 %shard_map.135 = s32[4,8,128]{2,1,0:T(8,128)} custom-call(s32[8,128]{1,0:T(8,128)} %broadcast_in_dim.83.flag_ref), custom_call_target="tpu_custom_call" | custom-call | tf_op jit(solution)/shard_map/pallas_call | solution.py:277
  14.6 0.9 slice_reduce_fusion
  15.5 0.7 fusion.4
  16.8 95.8 %conditional.1 = ((bf16[32,2,64,128]{3,2,1,0:T(8,128)(2,1)S(1)}, bf16[32,2,64,128]{3,2,1,0:T(8,128)(2,1)}, bf16[64,16,1024]{2,1,0:T(8,128)(2,1)S(1)})) conditional(s32[]{:T(128)} %clamp.3, (s32[6,128]{1,0:T(8,128)S(1)}, bf16[128,2,64,128]{3,2,1,0:T(8,128)(2,1)}, bf16[128,2,64,128]{3,2,1,0:T(8,128)(2,1)}, ...), branch_computations={%region_9.10_spmd, %region_10.11_spmd, %region_11.12_spmd, %region... | conditional | bytes 8 | solution.py:686
  16.8 95.7 %branch_0_fun.1 = (bf16[32,2,64,128]{3,2,1,0:T(8,128)(2,1)S(1)}, bf16[32,2,64,128]{3,2,1,0:T(8,128)(2,1)}, bf16[64,16,1024]{2,1,0:T(8,128)(2,1)S(1)}) custom-call(s32[6,128]{1,0:T(8,128)S(1)} %get-tuple-element.48.tab, bf16[128,2,64,128]{3,2,1,0:T(8,128)(2,1)} %get-tuple-element.110.keys_hbm, bf16[128,2,64,128]{3,2,1,0:T(8,128)(2,1)} %get-tuple-element.114.values_hbm, ...), custom_call_target="tpu_custom_call" | custom-call | tf_op jit(solution)/shard_map/cond/branch_0_fun/pallas_call | solution.py:627
  112.5 0.0 copy-start
  112.6 1.0 copy.58
  113.5 0.6 copy-done
  114.2 1.0 copy.59
  115.1 1.3 %copy.60 = bf16[64,16,1024]{2,1,0:T(8,128)(2,1)} copy(bf16[64,16,1024]{2,1,0:T(8,128)(2,1)S(1)} %get-tuple-element.156) | data formatting | bytes 4194304
  (3 shorter events, 0.0 us)
Async XLA Ops:
  112.5 1.6 %copy-start = (bf16[32,2,64,128]{3,2,1,0:T(8,128)(2,1)S(1)}, bf16[32,2,64,128]{3,2,1,0:T(8,128)(2,1)}, u32[]{:S(2)}) copy-start(bf16[32,2,64,128]{3,2,1,0:T(8,128)(2,1)} %get-tuple-element.155) | copy-start | bytes 3145732

commit v2 on v1

--- a/solution.py
+++ b/solution.py
@@ -243,7 +243,7 @@
 SEND_SPLIT = 2
 
 
-def flag_kernel(n, flag_ref, out_ref, send_sem, recv_sem):
+def prep_kernel(n, old_ref, slot_ref, len_ref, tab_ref, flag, got, send_sem, recv_sem):
     me = lax.axis_index("inst")
     barrier = pltpu.get_barrier_semaphore()
     for step in range(1, n):
@@ -253,12 +253,17 @@
             device_id={"inst": lax.rem(me + step, n)},
             device_id_type=pl.DeviceIdType.MESH,
         )
+    size = old_ref.shape[1]
+    wide = (size, size)
+    old = jnp.broadcast_to(old_ref[...], wide)
+    filled = jnp.max(old[:8].astype(jnp.float32), axis=1, keepdims=True) >= 0.0
+    flag[...] = jnp.broadcast_to(jnp.where(filled, me, 0), flag.shape)
     pl.semaphore_wait(barrier, n - 1)
     copies = []
     for step in range(1, n):
         copy = pltpu.make_async_remote_copy(
-            src_ref=flag_ref,
-            dst_ref=out_ref.at[step],
+            src_ref=flag,
+            dst_ref=got.at[step],
             send_sem=send_sem.at[step],
             recv_sem=recv_sem.at[step],
             device_id={"inst": lax.rem(me + step, n)},
@@ -266,45 +271,58 @@
         )
         copy.start()
         copies.append(copy)
-    out_ref[0] = flag_ref[...]
+
+    r = lax.broadcasted_iota(jnp.int32, wide, 0)
+    c = lax.broadcasted_iota(jnp.int32, wide, 1)
+
+    def total(where, what, axis):
+        return jnp.sum(jnp.where(where, what.astype(jnp.float32), 0.0), axis=axis, keepdims=True)
+
+    old_t = old.T
+    source = total(old_t == c, r, 0)
+    placed = total(old_t == c, jnp.broadcast_to(slot_ref[...], wide), 1).astype(jnp.int32)
+    placed = jnp.where(old_t >= 0, placed, -1)
+    by_slot = total(placed == c, r, 0)
+    length = jnp.broadcast_to(len_ref[...], wide)
+    length_t = length.T
+    counts = (length + (BLK - 1)) // BLK
+    counts_t = (length_t + (BLK - 1)) // BLK
+    ends = total(r <= c, counts_t, 0)
+    ends_t = total(c <= r, counts, 1).astype(jnp.int32)
+    starts_t = ends_t - counts_t
+    inside = (starts_t <= c) & (c < ends_t)
+    owner = total(inside, r, 0)
+    live = jnp.minimum(total(inside, length_t - (c - starts_t) * BLK, 0), float(BLK))
+    first = total(inside & (starts_t == c), jnp.ones(wide, jnp.int32), 0)
+    rows = [source, by_slot, owner, live, first, ends - 1.0]
+    for n_row, row in enumerate(rows):
+        tab_ref[n_row : n_row + 1, :] = row.astype(jnp.int32)
     for copy in copies:
         copy.wait()
-
-
-def find_holder(old_block, n):
-    me = lax.axis_index("inst")
-    mine = jnp.broadcast_to((jnp.max(old_block) >= 0).astype(jnp.int32), (8, 128))
-    flags = pl.pallas_call(
-        functools.partial(flag_kernel, n),
-        out_shape=jax.ShapeDtypeStruct((n, 8, 128), jnp.int32),
-        in_specs=[pl.BlockSpec(memory_space=pltpu.VMEM)],
-        out_specs=pl.BlockSpec(memory_space=pltpu.VMEM),
-        scratch_shapes=[pltpu.SemaphoreType.DMA((n,)), pltpu.SemaphoreType.DMA((n,))],
+    holder = flag[0:1, :]
+    for step in range(1, n):
+        holder = holder + got[step, 0:1, :]
+    tab_ref[6:7, :] = holder
+    tab_ref[7:8, :] = holder
+
+
+def prepare(old_block, new_slot, lengths, n):
+    size = new_slot.shape[0]
+    lengths = jnp.pad(lengths, (0, size - lengths.shape[0]))
+    vmem = pl.BlockSpec(memory_space=pltpu.VMEM)
+    return pl.pallas_call(
+        functools.partial(prep_kernel, n),
+        out_shape=jax.ShapeDtypeStruct((8, size), jnp.int32),
+        in_specs=[vmem] * 3,
+        out_specs=vmem,
+        scratch_shapes=[
+            pltpu.VMEM((8, size), jnp.int32),
+            pltpu.VMEM((n, 8, size), jnp.int32),
+            pltpu.SemaphoreType.DMA((n,)),
+            pltpu.SemaphoreType.DMA((n,)),
+        ],
         compiler_params=pltpu.CompilerParams(collective_id=0, has_side_effects=True),
-    )(mine)
-    origin = (me - jnp.arange(n, dtype=jnp.int32) + n) % n
-    return jnp.sum(origin * flags[:, 0, 0])
-
-
-def tables(old_block, new_slot, lengths):
-    blocks = new_slot.shape[0]
-    requests = lengths.shape[0]
-    ids = jnp.arange(blocks, dtype=jnp.int32)
-    spots = jnp.arange(old_block.shape[0], dtype=jnp.int32)
-    source = jnp.sum(jnp.where(old_block[None, :] == ids[:, None], spots[None, :], 0), axis=1)
-    placed = jnp.sum(jnp.where(old_block[:, None] == ids[None, :], new_slot[None, :] + 1, 0), axis=1) - 1
-    by_slot = jnp.sum(jnp.where(placed[None, :] == ids[:, None], spots[None, :], 0), axis=1)
-    counts = (lengths + BLK - 1) // BLK
-    reqs = jnp.arange(requests, dtype=jnp.int32)
-    ends = jnp.sum(jnp.where(reqs[None, :] <= reqs[:, None], counts[None, :], 0), axis=1)
-    starts = ends - counts
-    inside = (starts[None, :] <= ids[:, None]) & (ids[:, None] < ends[None, :])
-    owner = jnp.sum(jnp.where(inside, reqs[None, :], 0), axis=1)
-    left = lengths[None, :] - (ids[:, None] - starts[None, :]) * BLK
-    live = jnp.minimum(jnp.sum(jnp.where(inside, left, 0), axis=1), BLK)
-    first = jnp.sum(jnp.where(inside & (starts[None, :] == ids[:, None]), 1, 0), axis=1)
-    last = jnp.pad(ends - 1, (0, blocks - requests))
-    return jnp.stack([source, by_slot, owner, live, first, last])
+    )(old_block.reshape(1, size), new_slot.reshape(1, size), lengths.reshape(1, size))
 
 
 def fused_kernel(
@@ -366,9 +384,27 @@
         pl.semaphore_signal(
             barrier, inc=1, device_id={"inst": lax.rem(me + step, insts)}, device_id_type=mesh_id
         )
+
+    lanes = pl.ds(pl.multiple_of(head * head_dim, head_dim), head_dim)
+
+    loads = [
+        pltpu.make_async_copy(src, dst, load_sem.at[n])
+        for n, (src, dst) in enumerate(
+            (
+                (keys_hbm, kbuf),
+                (values_hbm, vbuf),
+                (queries_hbm, qbuf),
+                (dkeys_hbm.at[:, :, lanes], dk.at[pl.ds(holder * rows_loc, rows_loc)]),
+                (dvals_hbm.at[:, :, lanes], dv.at[pl.ds(holder * rows_loc, rows_loc)]),
+            )
+        )
+    ]
+
+    @pl.when(me == holder)
+    def _():
+        loads[0].start()
+
     pl.semaphore_wait(barrier, insts - 1)
-
-    lanes = pl.ds(pl.multiple_of(head * head_dim, head_dim), head_dim)
 
     def draft_copies(origin):
         rows = pl.ds(origin * rows_loc, rows_loc)
@@ -440,21 +476,6 @@
 
     @pl.when(me == holder)
     def _():
-        loads = [
-            pltpu.make_async_copy(src, dst, load_sem.at[n])
-            for n, (src, dst) in enumerate(
-                (
-                    (keys_hbm, kbuf),
-                    (values_hbm, vbuf),
-                    (queries_hbm, qbuf),
-                    (dkeys_hbm.at[:, :, lanes], dk.at[pl.ds(holder * rows_loc, rows_loc)]),
-                    (dvals_hbm.at[:, :, lanes], dv.at[pl.ds(holder * rows_loc, rows_loc)]),
-                )
-            )
-        ]
-        for load in loads:
-            load.start()
-
         def fill(src, dst, inst):
             def one(i, _):
                 slot = inst * per_inst + i
@@ -464,20 +485,23 @@
             lax.fori_loop(0, per_inst, one, 0)
 
         loads[0].wait()
+        loads[1].start()
         fill(kbuf, send_k, far)
         fill(kbuf, send_k, cross_x)
         for n in range(units):
             block_copy(far, n).start()
-        loads[1].wait()
-        fill(vbuf, send_v, far)
         fill(kbuf, send_k, cross_y)
-        for n in range(units, 2 * units):
-            block_copy(far, n).start()
-        fill(vbuf, send_v, cross_x)
-        fill(vbuf, send_v, cross_y)
         for n in range(SEND_SPLIT):
             block_copy(cross_x, n).start()
             block_copy(cross_y, n).start()
+        loads[1].wait()
+        for load in loads[2:]:
+            load.start()
+        fill(vbuf, send_v, far)
+        fill(vbuf, send_v, cross_x)
+        for n in range(units, 2 * units):
+            block_copy(far, n).start()
+        fill(vbuf, send_v, cross_y)
         fill(kbuf, send_k, holder)
         fill(vbuf, send_v, holder)
 
@@ -674,15 +698,15 @@
         and old_keys.shape[1] * old_keys.shape[2] == BLK
         and queries.shape[2] // old_keys.shape[3] == GROUP
         and lengths.shape[0] % 8 == 0
-        and new_slot.shape[0] % 16 == 0
+        and new_slot.shape[0] % BLK == 0
         and lengths.shape[0] <= new_slot.shape[0]
     )
     if not plain:
         return general_shards(
             old_keys, old_values, old_block, new_slot, lengths, queries, draft_keys, draft_values
         )
-    holder = find_holder(old_block, insts)
-    tab = tables(old_block, new_slot, lengths)
+    tab = prepare(old_block, new_slot, lengths, insts)
+    holder = tab[6, 0]
     return lax.switch(
         holder,
         [functools.partial(fused, h) for h in range(insts)],

time: 117 us -> 110 us (0.940)
  other arithmetic: 5.84 us -> 0 us
    reduce_sum x5 -> x0, other arithmetic: 2.54 us -> none  [the longest x1 0.91 us: tables(): jnp.sum(jnp.where(old_block[:, None] == ids[None, :], new_slot[None, :] +...]
    reduce_max x1 -> x0, other arithmetic: 1.29 us -> none  [find_holder(): jnp.max(old_block) >= 0]
where the time goes in v2:
time: 110 us; the launch traced here: 109 us
  Pallas kernels  103 us (94%)
  local copies, waits for them, and re-layouts  5.57 us (5%)
  between operations  1.31 us (1%)
    pallas_call x1, Pallas kernels, fused(): pl.pallas_call(functools.partial(fused_kernel, holder), out_shape=(jax.Sh...  95.7 us
    pallas_call x1, Pallas kernels, prepare(): pl.pallas_call(functools.partial(prep_kernel, n), out_shape=jax.ShapeDtyp...  6.88 us
    unnamed x5, local copies, waits for them, and re-layouts  3.88 us

profile of v2, /device:TPU:0, one launch (start us, length us, event | category | flops | bytes accessed | tf_op | source)
XLA Modules:
  0.0 109.5 jit_solution(13023730116752435714)
XLA Ops:
  0.6 1.2 %pad_bitcast_fusion.len_ref = s32[1,128]{1,0:T(1,128)} fusion(s32[64]{0:T(128)} %param.16), kind=kLoop, calls=%fused_computation | loop fusion | bytes 768 | tf_op jit(solution)/shard_map/reshape | solution.py:325
  1.8 6.9 %shard_map.115 = s32[8,128]{1,0:T(8,128)S(1)} custom-call(s32[1,128]{1,0:T(1,128)} %bitcast.5, s32[1,128]{1,0:T(1,128)} %bitcast.6, s32[1,128]{1,0:T(1,128)} %pad_bitcast_fusion.len_ref), custom_call_target="tpu_custom_call" | custom-call | tf_op jit(solution)/shard_map/pallas_call | solution.py:313
  8.7 0.5 slice.3
  9.9 95.7 %conditional.1 = ((bf16[32,2,64,128]{3,2,1,0:T(8,128)(2,1)S(1)}, bf16[32,2,64,128]{3,2,1,0:T(8,128)(2,1)}, bf16[64,16,1024]{2,1,0:T(8,128)(2,1)S(1)})) conditional(s32[]{:T(128)} %bitcast.3, (s32[8,128]{1,0:T(8,128)S(1)}, bf16[128,2,64,128]{3,2,1,0:T(8,128)(2,1)}, bf16[128,2,64,128]{3,2,1,0:T(8,128)(2,1)}, ...), branch_computations={%region_0.1_spmd, %region_1.2_spmd, %region_2.3_spmd, %region_3.4_... | conditional | bytes 8 | solution.py:710
  9.9 95.7 %branch_2_fun.1 = (bf16[32,2,64,128]{3,2,1,0:T(8,128)(2,1)S(1)}, bf16[32,2,64,128]{3,2,1,0:T(8,128)(2,1)}, bf16[64,16,1024]{2,1,0:T(8,128)(2,1)S(1)}) custom-call(s32[8,128]{1,0:T(8,128)S(1)} %get-tuple-element.60.tab, bf16[128,2,64,128]{3,2,1,0:T(8,128)(2,1)} %get-tuple-element.61.keys_hbm, bf16[128,2,64,128]{3,2,1,0:T(8,128)(2,1)} %get-tuple-element.62.values_hbm, ...), custom_call_target="tpu_custom_call" | custom-call | tf_op jit(solution)/shard_map/cond/branch_2_fun/pallas_call | solution.py:651
  105.6 0.0 copy-start
  105.6 1.0 copy.38
  106.6 0.6 copy-done
  107.2 1.0 copy.39
  108.2 1.3 %copy.40 = bf16[64,16,1024]{2,1,0:T(8,128)(2,1)} copy(bf16[64,16,1024]{2,1,0:T(8,128)(2,1)S(1)} %get-tuple-element.107) | data formatting | bytes 4194304
Async XLA Ops:
  105.6 1.6 %copy-start = (bf16[32,2,64,128]{3,2,1,0:T(8,128)(2,1)S(1)}, bf16[32,2,64,128]{3,2,1,0:T(8,128)(2,1)}, u32[]{:S(2)}) copy-start(bf16[32,2,64,128]{3,2,1,0:T(8,128)(2,1)} %get-tuple-element.106) | copy-start | bytes 3145732

commit v3 on v2

--- a/solution.py
+++ b/solution.py
@@ -240,10 +240,11 @@
 
 
 UNROLL = 4
+LIMIT = 60 * 1024 * 1024
 SEND_SPLIT = 2
 
 
-def prep_kernel(n, old_ref, slot_ref, len_ref, tab_ref, flag, got, send_sem, recv_sem):
+def prep_kernel(n, old_ref, slot_ref, len_ref, tab_ref, flag, got, padded, send_sem, recv_sem):
     me = lax.axis_index("inst")
     barrier = pltpu.get_barrier_semaphore()
     for step in range(1, n):
@@ -283,7 +284,9 @@
     placed = total(old_t == c, jnp.broadcast_to(slot_ref[...], wide), 1).astype(jnp.int32)
     placed = jnp.where(old_t >= 0, placed, -1)
     by_slot = total(placed == c, r, 0)
-    length = jnp.broadcast_to(len_ref[...], wide)
+    padded[...] = jnp.zeros(padded.shape, jnp.int32)
+    padded[0:1, : len_ref.shape[1]] = len_ref[...]
+    length = jnp.broadcast_to(padded[0:1, :], wide)
     length_t = length.T
     counts = (length + (BLK - 1)) // BLK
     counts_t = (length_t + (BLK - 1)) // BLK
@@ -308,7 +311,6 @@
 
 def prepare(old_block, new_slot, lengths, n):
     size = new_slot.shape[0]
-    lengths = jnp.pad(lengths, (0, size - lengths.shape[0]))
     vmem = pl.BlockSpec(memory_space=pltpu.VMEM)
     return pl.pallas_call(
         functools.partial(prep_kernel, n),
@@ -318,11 +320,12 @@
         scratch_shapes=[
             pltpu.VMEM((8, size), jnp.int32),
             pltpu.VMEM((n, 8, size), jnp.int32),
+            pltpu.VMEM((8, size), jnp.int32),
             pltpu.SemaphoreType.DMA((n,)),
             pltpu.SemaphoreType.DMA((n,)),
         ],
         compiler_params=pltpu.CompilerParams(collective_id=0, has_side_effects=True),
-    )(old_block.reshape(1, size), new_slot.reshape(1, size), lengths.reshape(1, size))
+    )(old_block.reshape(1, size), new_slot.reshape(1, size), lengths.reshape(1, lengths.shape[0]))
 
 
 def fused_kernel(
@@ -476,34 +479,37 @@
 
     @pl.when(me == holder)
     def _():
-        def fill(src, dst, inst):
+        def fill(inst, n):
+            src, dst = ((kbuf, send_k), (vbuf, send_v))[n // units]
+
             def one(i, _):
-                slot = inst * per_inst + i
+                slot = inst * per_inst + (n % units) * unit + i
                 dst[slot] = src[tab[1, slot]]
                 return 0
 
-            lax.fori_loop(0, per_inst, one, 0)
+            lax.fori_loop(0, unit, one, 0, unroll=4)
+
+        def stage(pairs):
+            for at, pair in enumerate(pairs):
+                fill(*pair)
+                if at >= 2:
+                    block_copy(*pairs[at - 2]).start()
+            for pair in pairs[-2:]:
+                block_copy(*pair).start()
 
         loads[0].wait()
         loads[1].start()
-        fill(kbuf, send_k, far)
-        fill(kbuf, send_k, cross_x)
-        for n in range(units):
-            block_copy(far, n).start()
-        fill(kbuf, send_k, cross_y)
-        for n in range(SEND_SPLIT):
-            block_copy(cross_x, n).start()
-            block_copy(cross_y, n).start()
+        early = [(inst, n) for n in range(SEND_SPLIT) for inst in (cross_x, cross_y)]
+        stage([(far, n) for n in range(units)] + early)
         loads[1].wait()
         for load in loads[2:]:
             load.start()
-        fill(vbuf, send_v, far)
-        fill(vbuf, send_v, cross_x)
-        for n in range(units, 2 * units):
-            block_copy(far, n).start()
-        fill(vbuf, send_v, cross_y)
-        fill(kbuf, send_k, holder)
-        fill(vbuf, send_v, holder)
+        stage([(far, n) for n in range(units, 2 * units)])
+        for n in range(SEND_SPLIT, 2 * units):
+            fill(cross_x, n)
+            fill(cross_y, n)
+        for n in range(2 * units):
+            fill(holder, n)
 
         for load in loads[2:]:
             load.wait()
@@ -685,7 +691,7 @@
             dma((8,)),
         ],
         compiler_params=pltpu.CompilerParams(
-            collective_id=1 + holder, has_side_effects=True, vmem_limit_bytes=60 * 1024 * 1024
+            collective_id=1 + holder, has_side_effects=True, vmem_limit_bytes=LIMIT
         ),
     )(tab, old_keys, old_values, queries, draft_keys, draft_values)
 

time: 110 us -> 108 us (0.982)
  local copies, waits for them, and re-layouts: 5.57 us -> 4.4 us
    reshape x1 -> x0, local copies, waits for them, and re-layouts: 1.17 us -> none  [prepare(): lengths.reshape(1, size)]
where the time goes in v3:
time: 108 us
  Pallas kernels  102 us (94%)
  local copies, waits for them, and re-layouts  4.4 us (4%)
  between operations  1.31 us (1%)
    pallas_call x1, Pallas kernels, fused(): pl.pallas_call(functools.partial(fused_kernel, holder), out_shape=(jax.Sh...  95.2 us
    pallas_call x1, Pallas kernels, prepare(): pl.pallas_call(functools.partial(prep_kernel, n), out_shape=jax.ShapeDtyp...  6.9 us
    unnamed x5, local copies, waits for them, and re-layouts  3.88 us

profile of v3, /device:TPU:0, one launch (start us, length us, event | category | flops | bytes accessed | tf_op | source)
XLA Modules:
  0.0 107.8 jit_solution(13935917360538739080)
XLA Ops:
  0.6 6.9 %shard_map.115 = s32[8,128]{1,0:T(8,128)S(1)} custom-call(s32[1,128]{1,0:T(1,128)} %bitcast.4, s32[1,128]{1,0:T(1,128)} %bitcast.5, s32[1,64]{1,0:T(1,128)} %bitcast.6), custom_call_target="tpu_custom_call" | custom-call | tf_op jit(solution)/shard_map/pallas_call | solution.py:315
  7.5 0.5 slice.3
  8.7 95.2 %conditional.1 = ((bf16[32,2,64,128]{3,2,1,0:T(8,128)(2,1)S(1)}, bf16[32,2,64,128]{3,2,1,0:T(8,128)(2,1)}, bf16[64,16,1024]{2,1,0:T(8,128)(2,1)S(1)})) conditional(s32[]{:T(128)} %bitcast.3, (s32[8,128]{1,0:T(8,128)S(1)}, bf16[128,2,64,128]{3,2,1,0:T(8,128)(2,1)}, bf16[128,2,64,128]{3,2,1,0:T(8,128)(2,1)}, ...), branch_computations={%region_0.0_spmd, %region_1.0_spmd, %region_2.0_spmd, %region_3.0_... | conditional | bytes 8 | solution.py:716
  8.7 95.2 %branch_1_fun.1 = (bf16[32,2,64,128]{3,2,1,0:T(8,128)(2,1)S(1)}, bf16[32,2,64,128]{3,2,1,0:T(8,128)(2,1)}, bf16[64,16,1024]{2,1,0:T(8,128)(2,1)S(1)}) custom-call(s32[8,128]{1,0:T(8,128)S(1)} %get-tuple-element.54.tab, bf16[128,2,64,128]{3,2,1,0:T(8,128)(2,1)} %get-tuple-element.55.keys_hbm, bf16[128,2,64,128]{3,2,1,0:T(8,128)(2,1)} %get-tuple-element.56.values_hbm, ...), custom_call_target="tpu_custom_call" | custom-call | tf_op jit(solution)/shard_map/cond/branch_1_fun/pallas_call | solution.py:657
  103.9 0.0 copy-start
  103.9 1.0 copy.38
  104.9 0.6 copy-done
  105.5 1.0 copy.39
  106.5 1.3 %copy.40 = bf16[64,16,1024]{2,1,0:T(8,128)(2,1)} copy(bf16[64,16,1024]{2,1,0:T(8,128)(2,1)S(1)} %get-tuple-element.107) | data formatting | bytes 4194304
Async XLA Ops:
  103.9 1.6 %copy-start = (bf16[32,2,64,128]{3,2,1,0:T(8,128)(2,1)S(1)}, bf16[32,2,64,128]{3,2,1,0:T(8,128)(2,1)}, u32[]{:S(2)}) copy-start(bf16[32,2,64,128]{3,2,1,0:T(8,128)(2,1)} %get-tuple-element.106) | copy-start | bytes 3145732
